TPU v7x, 32 devices: a whole 2x2x4 slice. The times are simulated.
32 devices in a mesh: seq: 8 (over z, y), chan: 4 (over x, core).
Axes of the slice: x: 2, y: 2, z: 4, core: 2. Of those that a mesh axis runs over, the one named last changes fastest.
Arguments:
- hidden_in: bfloat16 [1024, 2048], P('seq', 'chan'), may hold values from -6 to 6
- norm_gain: float32 [2048], replicated, may hold values from 0.5 to 1.5
- in_weight: bfloat16 [2048, 2, 4096], P('seq', None, 'chan'), may hold values from -0.125 to 0.125
- conv_weight: float32 [2, 4, 4096], P(None, None, 'chan'), may hold values from -3 to 3
- conv_bias: float32 [2, 4096], P(None, 'chan'), may hold values from -0.5 to 0.5
- proj_weight: bfloat16 [2, 4096, 160], P(None, 'chan'), may hold values from -0.1875 to 0.1875
- step_weight: bfloat16 [2, 128, 4096], P(None, None, 'chan'), may hold values from -0.5 to 0.5
- decay_rate: float32 [2, 4096], P(None, 'chan'), may hold values from 0.00024414062 to 0.25
- skip_gain: float32 [2, 4096], P(None, 'chan'), may hold values from 0.5 to 1.5
- out_weight: bfloat16 [4096, 2048], P('chan', 'seq'), may hold values from -0.09375 to 0.09375
Outputs:
- mixed: bfloat16 [1024, 2048], P('seq', 'chan')
All inputs are finite; a program needn't handle non-finite values.
Results may differ from a plain program's by a relative error of at most 0.0095.
Values may be sent and summed in bfloat16 or wider, within the bound.
No kernel may reach another device: no remote copies, remote signals or barrier semaphores. Data moves between devices by JAX's collectives and lax.ppermute only.
A program may use at most 128 MiB of HBM per device.

v0:
```python
import jax
import jax.numpy as jnp
from jax import lax
from jax.sharding import PartitionSpec as P

STATE = 16
WIDTH = 4


def with_halo(block, sides, width):
    for axis, dim in sides:
        count = lax.axis_size(axis)
        forward = [(i, i + 1) for i in range(count - 1)]
        backward = [(target, source) for source, target in forward]
        low = lax.ppermute(
            lax.slice_in_dim(block, block.shape[dim] - width, None, axis=dim), axis, forward
        )
        high = lax.ppermute(lax.slice_in_dim(block, 0, width, axis=dim), axis, backward)
        block = jnp.concatenate([low, block, high], axis=dim)
    return block


def entering(array, axis, combine, identity, reverse):
    devices, here = (lax.axis_size(axis), lax.axis_index(axis))
    everything = jax.tree.map(lambda part: lax.all_gather(part, axis), array)
    start = jax.tree.map(
        lambda part, zero: jnp.broadcast_to(jnp.asarray(zero, part.dtype), part.shape),
        array,
        identity,
    )

    def hop(k, before):
        at = devices - 1 - k if reverse else k
        reached = at > here if reverse else at < here
        new = combine(before, jax.tree.map(lambda part: part[at], everything))
        return jax.tree.map(lambda a, b: jnp.where(reached, a, b), new, before)

    return lax.fori_loop(0, devices, hop, start)


def conv_taps(padded, conv_weight, conv_bias, length):
    reach = conv_weight.shape[1] - 1
    forward = jnp.zeros((length, padded.shape[1]), jnp.float32) + conv_bias[0][None, :]
    backward = jnp.zeros((length, padded.shape[1]), jnp.float32) + conv_bias[1][None, :]
    for offset in range(reach + 1):
        forward = forward + conv_weight[0, offset][None, :] * padded[offset : offset + length]
        begin = 2 * reach - offset
        backward = backward + conv_weight[1, offset][None, :] * padded[begin : begin + length]
    return jax.nn.silu(jnp.stack([forward, backward])).astype(jnp.bfloat16)


def sweep(drive_values, key_rows, query_rows, epsilon, initial, reverse, keeping):
    product = jnp.ones(initial.shape, jnp.float32)

    def advance(carry, current):
        product, state = carry
        drive_row, key_row, query_row, eps_row = current
        decay = 1.0 - eps_row[None, :] * (key_row * key_row)[:, None]
        state = decay * state + key_row[:, None] * (eps_row * drive_row)[None, :]
        product = decay * product
        if keeping == "reads":
            output = jnp.sum(query_row[:, None] * state, axis=0)
        else:
            output = None
        return ((product, state), output)

    (product, state), outputs = lax.scan(
        advance,
        (product, initial),
        (drive_values, key_rows, query_rows, epsilon),
        reverse=reverse,
        unroll=16,
    )
    return (product, state, outputs)


def combine(earlier, latter):
    return (latter[0] * earlier[0], latter[0] * earlier[1] + latter[1])


def per_device(
    hidden_in,
    norm_gain,
    in_weight,
    conv_weight,
    conv_bias,
    proj_weight,
    step_weight,
    decay_rate,
    skip_gain,
    out_weight,
):
    gathered = lax.all_gather(hidden_in, "chan", axis=1, tiled=True).astype(jnp.float32)
    normed = (
        gathered
        * lax.rsqrt(jnp.mean(gathered * gathered, axis=1, keepdims=True) + 1e-05)
        * norm_gain[None, :]
    ).astype(jnp.bfloat16)
    row_count = normed.shape[0]
    channels = in_weight.shape[2]
    piece = lax.all_gather(in_weight, "seq", axis=0, tiled=True)
    projected = jnp.dot(
        normed, piece.reshape(piece.shape[0], 2 * channels), preferred_element_type=jnp.float32
    )
    projected = projected.astype(jnp.bfloat16).reshape(row_count, 2, channels)
    branch = projected[:, 0, :]
    gate_half = projected[:, 1, :].astype(jnp.float32)
    padded = with_halo(branch, (("seq", 0),), WIDTH - 1).astype(jnp.float32)
    driven = conv_taps(padded, conv_weight, conv_bias, row_count)
    partial_value = jnp.einsum(
        "dte,def->tdf", driven, proj_weight, preferred_element_type=jnp.float32
    )
    features = lax.psum(partial_value, "chan")
    key_rows = features[:, :, :STATE]
    query_rows = features[:, :, STATE : 2 * STATE]
    low_rank = features[:, :, 2 * STATE :].astype(jnp.bfloat16)
    step_size = jnp.einsum(
        "tdr,dre->tde", low_rank, step_weight, preferred_element_type=jnp.float32
    )
    beta_rows = 2.0 * decay_rate[None, :, :] * jax.nn.sigmoid(step_size)
    epsilon = beta_rows / (1.0 + beta_rows * jnp.sum(key_rows * key_rows, axis=2, keepdims=True))
    drive_values = driven.astype(jnp.float32)
    zero_state = jnp.zeros((STATE, channels), jnp.float32)
    keeping = "summary"
    passes = [
        sweep(
            drive_values[direction],
            key_rows[:, direction],
            query_rows[:, direction],
            epsilon[:, direction],
            zero_state,
            direction == 1,
            keeping,
        )
        for direction in range(2)
    ]
    identity = (jnp.ones((STATE, channels), jnp.float32), zero_state)
    incoming_forward = entering((passes[0][0], passes[0][1]), "seq", combine, identity, False)[1]
    incoming_reverse = entering((passes[1][0], passes[1][1]), "seq", combine, identity, True)[1]
    incoming = [incoming_forward, incoming_reverse]
    total = jnp.zeros((row_count, channels), jnp.float32)
    for direction in range(2):
        reads = sweep(
            drive_values[direction],
            key_rows[:, direction],
            query_rows[:, direction],
            epsilon[:, direction],
            incoming[direction],
            direction == 1,
            "reads",
        )[2]
        total = total + reads + skip_gain[direction][None, :] * drive_values[direction]
    combined = (total * jax.nn.silu(gate_half)).astype(jnp.bfloat16)
    partial_out = jnp.dot(
        combined,
        lax.all_gather(out_weight, "seq", axis=1, tiled=True),
        preferred_element_type=jnp.float32,
    )
    summed = lax.psum(partial_out, "chan")
    share_width = summed.shape[1] // lax.axis_size("chan")
    share = lax.dynamic_slice_in_dim(summed, lax.axis_index("chan") * share_width, share_width, 1)
    return share.astype(jnp.bfloat16)


def solution(mesh):
    in_specs = (
        P("seq", "chan"),
        P(),
        P("seq", None, "chan"),
        P(None, None, "chan"),
        P(None, "chan"),
        P(None, "chan", None),
        P(None, None, "chan"),
        P(None, "chan"),
        P(None, "chan"),
        P("chan", "seq"),
    )
    out_specs = P("seq", "chan")
    return jax.shard_map(
        per_device, mesh=mesh, in_specs=in_specs, out_specs=out_specs, check_vma=False
    )
```

profile of v0, /device:TPU:0, one launch (start us, length us, event | category | flops | bytes accessed | tf_op | source)
XLA Modules:
  0.0 489.7 jit_solution(10717089666315897083)
XLA Ops:
  7.3 8.9 %all_gather.33 = bf16[128,2048]{1,0:T(8,128)(2,1)S(1)} all-gather(bf16[128,512]{1,0:T(8,128)(2,1)} %param.22), channel_id=1, replica_groups=mesh['seq'=8,'chan'=4] {'chan'}, dimensions={1}, use_global_device_ids=true | all-gather | bytes 655360 | tf_op jit(solution)/shard_map/all_gather | solution.py:93
  18.1 118.6 %all-gather.7.cloned.1.call-done = bf16[2048,2,1024]{2,1,0:T(2,128)(2,1)} async-done(((bf16[256,2,1024]{2,1,0:T(2,128)(2,1)}), bf16[2048,2,1024]{2,1,0:T(2,128)(2,1)}) %all-gather.7.cloned.1.call-update) | async-done | bytes 8388624 | tf_op jit(solution)/shard_map/all_gather | solution.py:101
  136.7 10.1 %copy.42 = bf16[256,8,2,1024]{3,1,2,0:T(8,128)(2,1)} copy(bf16[256,8,2,1024]{3,2,1,0:T(2,128)(2,1)} %bitcast.855) | data formatting | bytes 16777216
  146.8 4.7 convolution_convert_fusion
  153.3 4.5 collective-permute-start
  163.2 30.7 %all-reduce.3.cloned.1.call-done = f32[128,2,160]{0,2,1:T(8,128)} async-done(((f32[128,2,160]{0,2,1:T(8,128)}), f32[128,2,160]{0,2,1:T(8,128)}) %all-reduce.3.cloned.1.call-update) | async-done | bytes 163856 | tf_op jit(solution)/shard_map/psum | solution.py:113
  199.1 22.7 %while.92 = (s32[]{:T(128)}, f32[16,1024]{1,0:T(8,128)S(1)}, f32[16,1024]{1,0:T(8,128)S(1)}, f32[8,16,1024]{2,1,0:T(8,128)}, f32[8,16,16]{2,1,0:T(8,128)S(1)}, /...) while((s32[]{:T(128)}, f32[16,1024]{1,0:T(8,128)S(1)}, ...), condition=%wide.region_26.27_spmd.clone, body=%wide.region_25.26_spmd.clone.sunk | while | flops 2146579 | bytes 924200 | solution.py:67
  199.1 2.0 constant_dynamic-slice_fusion.231
  202.1 2.0 constant_dynamic-slice_fusion.231
  207.8 1.8 constant_dynamic-slice_fusion.231
  210.6 2.0 constant_dynamic-slice_fusion.231
  213.5 2.0 constant_dynamic-slice_fusion.231
  219.2 1.8 constant_dynamic-slice_fusion.231
  221.8 9.5 %while.90 = (s32[]{:T(128)}, f32[16,1024]{1,0:T(8,128)S(1)}, f32[16,1024]{1,0:T(8,128)S(1)}, f32[8,16,1024]{2,1,0:T(8,128)S(1)}, f32[8,16,16]{2,1,0:T(8,128)S(1)...) while((s32[]{:T(128)}, f32[16,1024]{1,0:T(8,128)S(1)}, ...), condition=%wide.region_4.5_spmd.clone, body=%wide.region_3.4_spmd.clone.sunk | while | flops 2146578 | bytes 924180 | solution.py:67
  231.3 37.0 %all-gather.1 = f32[128,1024]{1,0:T(8,128)} all-gather(f32[16,1024]{1,0:T(8,128)S(1)} %get-tuple-element.566), channel_id=3, replica_groups=mesh['seq'=8,'chan'=4] {'seq'}, dimensions={0}, use_global_device_ids=true | all-gather | bytes 589824 | tf_op jit(solution)/shard_map/all_gather | solution.py:25
  268.3 34.7 %all-gather.3 = f32[128,1024]{1,0:T(8,128)} all-gather(f32[16,1024]{1,0:T(8,128)S(1)} %get-tuple-element.570), channel_id=5, replica_groups=mesh['seq'=8,'chan'=4] {'seq'}, dimensions={0}, use_global_device_ids=true | all-gather | bytes 589824 | tf_op jit(solution)/shard_map/all_gather | solution.py:25
  303.0 33.4 %all-gather = f32[128,1024]{1,0:T(8,128)} all-gather(f32[16,1024]{1,0:T(8,128)S(1)} %get-tuple-element.565), channel_id=2, replica_groups=mesh['seq'=8,'chan'=4] {'seq'}, dimensions={0}, use_global_device_ids=true | all-gather | bytes 589824 | tf_op jit(solution)/shard_map/all_gather | solution.py:25
  336.4 7.5 %while.91 = (s32[]{:T(128)}, f32[16,1024]{1,0:T(8,128)S(1)}, s32[]{:T(128)}, f32[8,16,1024]{2,1,0:T(8,128)}, f32[8,16,1024]{2,1,0:T(8,128)}, /*index=5*/s32[]{:T(128)}, s32[]{:T(128)}) while((s32[]{:T(128)}, f32[16,1024]{1,0:T(8,128)S(1)}, s32[]{:T(128)}, f32[8,16,1024]{2,1,0:T(8,128)}, f32[8,16,1024]{2,1,0:T(8,128)}, ...), condition=%wide.region_6.7_spmd.clone, body=%wide.region_5.6_spmd.clone.sunk | while | flops 65540 | bytes 262253 | solution.py:38
  343.9 33.6 %all-gather.2 = f32[128,1024]{1,0:T(8,128)} all-gather(f32[16,1024]{1,0:T(8,128)S(1)} %get-tuple-element.569), channel_id=4, replica_groups=mesh['seq'=8,'chan'=4] {'seq'}, dimensions={0}, use_global_device_ids=true | all-gather | bytes 589824 | tf_op jit(solution)/shard_map/all_gather | solution.py:25
  377.5 7.5 %while.93 = (s32[]{:T(128)}, f32[16,1024]{1,0:T(8,128)S(1)}, s32[]{:T(128)}, f32[8,16,1024]{2,1,0:T(8,128)}, f32[8,16,1024]{2,1,0:T(8,128)}, /*index=5*/s32[]{:T(128)}, s32[]{:T(128)}, s32[]{:T(128)}, s32[]{:T(128)}) while((s32[]{:T(128)}, f32[16,1024]{1,0:T(8,128)S(1)}, s32[]{:T(128)}, f32[8,16,1024]{2,1,0:T(8,128)}, ...), condition=%wide.region_28.29_spmd.clone, body=%wide.region_27.28_spmd.clone.sunk | while | flops 65544 | bytes 262315 | solution.py:38
  385.9 33.0 %while.89 = (s32[]{:T(128)}, f32[16,1024]{1,0:T(8,128)S(1)}, f32[8,16,1024]{2,1,0:T(8,128)}, f32[8,16,1024]{2,1,0:T(8,128)}, f32[8,16,16]{2,1,0:T(8,128)S(1)}, /...) while((s32[]{:T(128)}, f32[16,1024]{1,0:T(8,128)S(1)}, ...), condition=%wide.region_46.47_spmd, body=%wide.region_29.46_spmd.sunk | while | flops 2408722 | bytes 2033121 | solution.py:67
  386.1 2.0 constant_dynamic-slice_fusion.229
  390.3 2.0 constant_dynamic-slice_fusion.229
  394.6 1.8 constant_dynamic-slice_fusion.229
  398.6 1.8 constant_dynamic-slice_fusion.229
  402.6 2.0 constant_dynamic-slice_fusion.229
  406.8 2.0 constant_dynamic-slice_fusion.229
  411.0 1.8 constant_dynamic-slice_fusion.229
  415.0 1.8 constant_dynamic-slice_fusion.229
  418.9 32.4 %while.88 = (s32[]{:T(128)}, f32[16,1024]{1,0:T(8,128)S(1)}, f32[8,16,1024]{2,1,0:T(8,128)S(1)}, f32[8,16,1024]{2,1,0:T(8,128)S(1)}, f32[8,16,16]{2,1,0:T(8,128)...) while((s32[]{:T(128)}, f32[16,1024]{1,0:T(8,128)S(1)}, ...), condition=%wide.region_24.25_spmd, body=%wide.region_7.24_spmd.sunk | while | flops 2490641 | bytes 2106965 | solution.py:67
  452.8 2.9 fusion.342
  455.7 26.7 %all-reduce.4 = bf16[128,2048]{1,0:T(8,128)(2,1)S(1)} all-reduce(f32[128,2048]{1,0:T(8,128)S(1)} %fusion.342), channel_id=1, replica_groups=mesh['seq'=8,'chan'=4] {'chan'}, use_global_device_ids=true, to_apply=%region_47.48 | all-reduce | flops 262144 | bytes 1572864 | tf_op jit(solution)/shard_map/psum | solution.py:159
  (853 shorter events, 97.4 us)
Async XLA Ops:
  6.5 153.8 %copy-start = (bf16[2,1024,160]{1,2,0:T(8,128)(2,1)S(1)}, bf16[2,1024,160]{1,2,0:T(8,128)(2,1)}, u32[]{:S(2)}) copy-start(bf16[2,1024,160]{1,2,0:T(8,128)(2,1)} %param.27) | copy-start | bytes 1966084
  6.5 130.2 %all-gather.7.cloned.1.call-start = ((), (), s32[]{:S(2)}) async-start(), calls=%async_computation | async-start | bytes 9437184 | tf_op jit(solution)/shard_map/all_gather | solution.py:101
  7.3 186.6 %all-reduce.3.cloned.1.call-start = ((), (), s32[]{:S(2)}) async-start(), calls=%async_computation.1 | async-start | bytes 327680 | tf_op jit(solution)/shard_map/psum | solution.py:113
  136.7 10.1 %copy-start.4 = (f32[2048]{0:T(1024)S(1)}, f32[2048]{0:T(1024)}, u32[]{:S(2)}) copy-start(f32[2048]{0:T(1024)} %param.23) | copy-start | bytes 24580
  151.5 10.6 %copy-start.5 = (f32[2,1024]{1,0:T(2,128)S(1)}, f32[2,1024]{1,0:T(2,128)}, u32[]{:S(2)}) copy-start(f32[2,1024]{1,0:T(2,128)} %param.29) | copy-start | bytes 24580
  151.5 10.7 %copy-start.6 = (f32[2,1024]{1,0:T(2,128)S(1)}, f32[2,1024]{1,0:T(2,128)}, u32[]{:S(2)}) copy-start(f32[2,1024]{1,0:T(2,128)} %param.30) | copy-start | bytes 24580
  152.0 7.5 %collective-permute-start.1 = (bf16[3,1024]{1,0:T(4,128)(2,1)S(1)}, bf16[3,1024]{1,0:T(4,128)(2,1)S(1)}, u32[]{:S(2)}, u32[]{:S(2)}) collective-permute-start(bf16[3,1024]{1,0:T(4,128)(2,1)S(1)} %bitcast.1151), channel_id=1, source_target_pairs={{4,0},{8,4},{12,8},{16,12},{20,16},{24,20},{28,24},{5,1},{9,5},{13... | collective-permute-start | bytes 18440 | tf_op jit(solution)/shard_map/ppermute | solution.py:18
  153.3 6.2 %collective-permute-start = (bf16[3,1024]{1,0:T(4,128)(2,1)S(1)}, bf16[3,1024]{1,0:T(4,128)(2,1)S(1)}, u32[]{:S(2)}, u32[]{:S(2)}) collective-permute-start(bf16[3,1024]{1,0:T(4,128)(2,1)S(1)} %bitcast.1150), channel_id=1, source_target_pairs={{0,4},{4,8},{8,12},{12,16},{16,20},{20,24},{24,28},{1,5},{5,9},{9,... | collective-permute-start | bytes 18440 | tf_op jit(solution)/shard_map/ppermute | solution.py:15
  161.4 291.4 %all-gather.9.cloned.1.call-start = ((), (), s32[]{:S(2)}) async-start(), calls=%async_computation.2 | async-start | bytes 4718592 | tf_op jit(solution)/shard_map/all_gather | solution.py:156
  163.2 35.9 %copy-start.1 = (f32[16,1024]{1,0:T(8,128)S(1)}, f32[16,1024]{1,0:T(8,128)}, u32[]{:S(2)}) copy-start(f32[16,1024]{1,0:T(8,128)} %custom-call.4) | copy-start | bytes 196612
  163.2 35.9 %copy-start.2 = (f32[16,1024]{1,0:T(8,128)S(1)}, f32[16,1024]{1,0:T(8,128)}, u32[]{:S(2)}) copy-start(f32[16,1024]{1,0:T(8,128)} %custom-call.3) | copy-start | bytes 196612
  231.3 154.6 %copy-start.3 = (f32[8,16,16]{2,1,0:T(8,128)}, f32[8,16,16]{2,1,0:T(8,128)S(1)}, u32[]{:S(2)}) copy-start(f32[8,16,16]{2,1,0:T(8,128)S(1)} %get-tuple-element.2563) | copy-start | bytes 24580
Sparse Core Ops, SparseCore 0:
  9.5 127.1 all-gather.6
  161.5 32.3 all-reduce.2
  195.9 86.4 all-gather.8
where the time goes:
time: 494 us; the launch traced here: 490 us
  blocking collectives  174 us (35%)
  waiting for transfers between devices  151 us (31%)
  local copies, waits for them, and re-layouts  69.2 us (14%)
  other arithmetic  59.8 us (12%)
  between operations  13.4 us (3%)
  matrix products  10.3 us (2%)
  loops' own time  6.06 us (1%)
  starting transfers between devices  5.92 us (1%)
    all_gather x4, blocking collectives, entering(): everything = jax.tree.map(lambda part: lax.all_gather(part, axis), array)  139 us
    all_gather x1, waiting for transfers between devices, per_device(): piece = lax.all_gather(in_weight, 'seq', axis=0, tiled=True)  119 us
    slice x32, local copies, waits for them, and re-layouts, sweep(): lax.scan(advance, (product, initial), (drive_values, key_rows, query_rows...  34.3 us
    psum x1, waiting for transfers between devices, per_device(): features = lax.psum(partial_value, 'chan')  30.7 us
    psum x1, blocking collectives, per_device(): summed = lax.psum(partial_out, 'chan')  26.7 us
    reduce_sum x136, other arithmetic, advance(): output = jnp.sum(query_row[:, None] * state, axis=0)  17.7 us
    select_n x16, other arithmetic, hop(): return jax.tree.map(lambda a, b: jnp.where(reached, a, b), new, before)  14.6 us
    mul x32, other arithmetic, advance(): decay = 1.0 - eps_row[None, :] * (key_row * key_row)[:, None]  12.7 us
  transfers between devices with their start and end apart: 5, of which 2 were waited for; matrix products, arithmetic and copies ran while one was open for 24% of the time, Pallas kernels for 0%

commit v1 on v0

v1 whole, which is shorter than its diff:
```python
import jax
import jax.numpy as jnp
from jax import lax
from jax.experimental import pallas as pl
from jax.experimental.pallas import tpu as pltpu
from jax.sharding import PartitionSpec as P

STATE = 16
WIDTH = 4
LANES = 128
UNROLL = 4


def swap(array, axis, distance):
    count = lax.axis_size(axis)
    return lax.ppermute(array, axis, [(i, i ^ distance) for i in range(count)])


def halo(branch, axis, width):
    count = lax.axis_size(axis)
    forward = [(i, i + 1) for i in range(count - 1)]
    backward = [(target, source) for source, target in forward]
    low = lax.ppermute(branch[:, -width:], axis, forward)
    high = lax.ppermute(branch[:, :width], axis, backward)
    return low, high


def conv_kernel(branch, low, high, weight, bias, proj, driven, features, padded):
    blocks, length, _ = branch.shape
    reach = WIDTH - 1
    first = 8 - reach
    partial = [jnp.zeros(features.shape[1:], jnp.float32) for _ in range(2)]
    for b in range(blocks):
        padded[8 : 8 + length] = branch[b].astype(jnp.float32)
        padded[first:8] = low[b].astype(jnp.float32)
        padded[8 + length : 8 + length + reach] = high[b].astype(jnp.float32)
        for d in range(2):
            total = jnp.broadcast_to(bias[d, b : b + 1], (length, LANES))
            for j in range(WIDTH):
                begin = first + (j if d == 0 else 2 * reach - j)
                total = total + weight[d, j, b : b + 1] * padded[begin : begin + length]
            value = (total / (1.0 + jnp.exp(-total))).astype(jnp.bfloat16)
            driven[d, b] = value
            partial[d] = partial[d] + jnp.dot(
                value, proj[d, b], preferred_element_type=jnp.float32
            )
    for d in range(2):
        features[d] = partial[d]


def spread(target, features, d, start):
    length = features.shape[1]
    for n in range(STATE):
        column = features[d, :, start + n : start + n + 1]
        target[:, n] = jnp.broadcast_to(column, (length, LANES))


def steps(length, reverse, body, carry):
    def many(i, carry):
        for j in range(UNROLL):
            t = i * UNROLL + j
            carry = body(length - 1 - t if reverse else t, carry)
        return carry

    return lax.fori_loop(0, length // UNROLL, many, carry)


def summary_kernel(driven, features, step_weight, rate, eps, drive, product, state, keys):
    _, blocks, length, _ = driven.shape
    for d in range(2):
        key = features[d, :, :STATE]
        square = jnp.sum(key * key, axis=1, keepdims=True)
        low = features[d, :, 2 * STATE :].astype(jnp.bfloat16)
        for b in range(blocks):
            step = jnp.dot(
                low, step_weight[d, :, b * LANES : (b + 1) * LANES],
                preferred_element_type=jnp.float32,
            )
            beta = 2.0 * rate[d, b : b + 1] / (1.0 + jnp.exp(-step))
            value = beta / (1.0 + beta * square)
            eps[d, :, b] = value
            drive[d, :, b] = value * driven[d, b].astype(jnp.float32)
        spread(keys, features, d, 0)

        def body(t, carry):
            products, states = carry
            e, x = eps[d, t], drive[d, t]
            new_products, new_states = [], []
            for n in range(STATE):
                k = jnp.broadcast_to(keys[t, n : n + 1], (blocks, LANES))
                decay = 1.0 - e * (k * k)
                new_products.append(products[n] * decay)
                new_states.append(states[n] * decay + k * x)
            return tuple(new_products), tuple(new_states)

        one = tuple(jnp.ones((blocks, LANES), jnp.float32) for _ in range(STATE))
        zero = tuple(jnp.zeros((blocks, LANES), jnp.float32) for _ in range(STATE))
        products, states = steps(length, d == 1, body, (one, zero))
        for n in range(STATE):
            product[d, n] = products[n].astype(product.dtype)
            state[d, n] = states[n].astype(state.dtype)


def read_kernel(driven, features, eps, drive, initial, gate, skip, out, keys, queries, total):
    _, blocks, length, _ = driven.shape
    for d in range(2):
        spread(keys, features, d, 0)
        spread(queries, features, d, STATE)

        def body(t, states):
            e, x = eps[d, t], drive[d, t]
            new_states = []
            reads = [None] * 4
            for n in range(STATE):
                k = jnp.broadcast_to(keys[t, n : n + 1], (blocks, LANES))
                q = jnp.broadcast_to(queries[t, n : n + 1], (blocks, LANES))
                state = states[n] * (1.0 - e * (k * k)) + k * x
                new_states.append(state)
                part = q * state
                reads[n % 4] = part if reads[n % 4] is None else reads[n % 4] + part
            read = (reads[0] + reads[1]) + (reads[2] + reads[3])
            total[t] = read if d == 0 else total[t] + read
            return tuple(new_states)

        steps(length, d == 1, body, tuple(initial[d, n] for n in range(STATE)))
    for b in range(blocks):
        g = gate[b].astype(jnp.float32)
        reads = total[:, b]
        for d in range(2):
            reads = reads + skip[d, b : b + 1] * driven[d, b].astype(jnp.float32)
        out[:, b * LANES : (b + 1) * LANES] = (reads * (g / (1.0 + jnp.exp(-g)))).astype(
            jnp.bfloat16
        )


def whole(count):
    return [pl.BlockSpec(memory_space=pltpu.VMEM) for _ in range(count)]


def kernel(body, args, shapes, scratch, name):
    return pl.pallas_call(
        body,
        out_shape=[jax.ShapeDtypeStruct(shape, dtype) for shape, dtype in shapes],
        in_specs=whole(len(args)),
        out_specs=whole(len(shapes)),
        scratch_shapes=[pltpu.VMEM(shape, dtype) for shape, dtype in scratch],
        name=name,
    )(*args)


def incoming(product, state):
    count, here = lax.axis_size("seq"), lax.axis_index("seq")
    both = jnp.stack([product, state], 1)
    slots = [None]
    for shift in range(1, count):
        payload = jnp.where(here + shift < count, both[0], both[1])
        slots.append(
            lax.ppermute(payload, "seq", [(i, (i + shift) % count) for i in range(count)])
        )
    result = []
    for d in range(2):
        entering = jnp.zeros(state.shape[1:], jnp.float32)
        passed = jnp.ones(state.shape[1:], jnp.float32)
        for distance in range(1, count):
            slot = slots[distance] if d == 0 else slots[count - distance]
            slot = slot.astype(jnp.float32)
            reached = here >= distance if d == 0 else here + distance < count
            entering = entering + jnp.where(reached, passed * slot[1], 0.0)
            passed = passed * slot[0]
        result.append(entering)
    return jnp.stack(result)


def scatter_sum(partial, axis):
    count, here = lax.axis_size(axis), lax.axis_index(axis)
    rows = partial.shape[0]
    half = 1
    left = count
    parts = partial.reshape(rows, count, -1)
    while left > 1:
        bit = (here // half) % 2
        parts = parts.reshape(rows, left // 2, 2, -1)
        kept = lax.dynamic_index_in_dim(parts, bit, 2, keepdims=False)
        sent = lax.dynamic_index_in_dim(parts, 1 - bit, 2, keepdims=False)
        if left == 2:
            sent = sent.astype(jnp.bfloat16)
        parts = kept + swap(sent, axis, half).astype(jnp.float32)
        half *= 2
        left //= 2
    return parts.reshape(rows, -1)


def per_device(
    hidden_in,
    norm_gain,
    in_weight,
    conv_weight,
    conv_bias,
    proj_weight,
    step_weight,
    decay_rate,
    skip_gain,
    out_weight,
):
    gathered = lax.all_gather(hidden_in, "chan", axis=1, tiled=True).astype(jnp.float32)
    normed = (
        gathered
        * lax.rsqrt(jnp.mean(gathered * gathered, axis=1, keepdims=True) + 1e-05)
        * norm_gain[None, :]
    ).astype(jnp.bfloat16)
    length = normed.shape[0]
    channels = in_weight.shape[2]
    blocks = channels // LANES
    piece = lax.all_gather(in_weight, "seq", axis=0, tiled=True)
    projected = jnp.dot(
        normed, piece.reshape(piece.shape[0], 2 * channels), preferred_element_type=jnp.float32
    ).astype(jnp.bfloat16)
    projected = projected.reshape(length, 2, blocks, LANES).transpose(1, 2, 0, 3)
    branch, gate = projected[0], projected[1]
    low, high = halo(branch, "seq", WIDTH - 1)
    tail = (blocks, LANES)
    bf16, f32 = jnp.bfloat16, jnp.float32
    driven, features = kernel(
        conv_kernel,
        (
            branch,
            low,
            high,
            conv_weight.reshape(2, WIDTH, *tail),
            conv_bias.reshape(2, *tail),
            proj_weight.reshape(2, blocks, LANES, -1),
        ),
        [((2, blocks, length, LANES), bf16), ((2, length, proj_weight.shape[2]), f32)],
        [((length + 16, LANES), f32)],
        "conv",
    )
    distance = 1
    while distance < lax.axis_size("chan"):
        features = features + swap(features, "chan", distance)
        distance *= 2
    spread_shape = ((length, STATE, LANES), f32)
    eps, drive, product, state = kernel(
        summary_kernel,
        (driven, features, step_weight, decay_rate.reshape(2, *tail)),
        [((2, length, *tail), f32)] * 2 + [((2, STATE, *tail), bf16)] * 2,
        [spread_shape],
        "summary",
    )
    initial = incoming(product, state)
    (combined,) = kernel(
        read_kernel,
        (driven, features, eps, drive, initial, gate, skip_gain.reshape(2, *tail)),
        [((length, channels), bf16)],
        [spread_shape] * 2 + [((length, *tail), f32)],
        "read",
    )
    partial_out = jnp.dot(
        combined,
        lax.all_gather(out_weight, "seq", axis=1, tiled=True),
        preferred_element_type=jnp.float32,
    )
    return scatter_sum(partial_out, "chan").astype(jnp.bfloat16)


def solution(mesh):
    in_specs = (
        P("seq", "chan"),
        P(),
        P("seq", None, "chan"),
        P(None, None, "chan"),
        P(None, "chan"),
        P(None, "chan", None),
        P(None, None, "chan"),
        P(None, "chan"),
        P(None, "chan"),
        P("chan", "seq"),
    )
    out_specs = P("seq", "chan")
    return jax.shard_map(
        per_device, mesh=mesh, in_specs=in_specs, out_specs=out_specs, check_vma=False
    )
```

time: 494 us -> 250 us (0.51)
  blocking collectives: 174 us -> 8.86 us
  other arithmetic: 59.8 us -> 4.46 us
  local copies, waits for them, and re-layouts: 69.2 us -> 17.7 us
  Pallas kernels: 0 us -> 24.2 us
  starting transfers between devices: 5.92 us -> 18.8 us
  loops' own time: 6.06 us -> 0 us
    all_gather x4 -> x0, blocking collectives: 139 us -> none  [entering(): everything = jax.tree.map(lambda part: lax.all_gather(part, axis), array)]
    slice x40 -> x1, local copies, waits for them, and re-layouts: 40.2 us -> 0.01 us  [halo(): high = lax.ppermute(branch[:, :width], axis, backward)]
    ppermute x2 -> x13, waiting for transfers between devices: 0.01 us -> 32.8 us  [the longest x7 16.7 us: incoming(): lax.ppermute(payload, 'seq', [(i, (i + shift) % count) for i in range(cou...]
    psum x1 -> x0, waiting for transfers between devices: 30.7 us -> none  [per_device(): features = lax.psum(partial_value, 'chan')]
    psum x1 -> x0, blocking collectives: 26.7 us -> none  [per_device(): summed = lax.psum(partial_out, 'chan')]
    pallas_call x0 -> x3, Pallas kernels: none -> 24.2 us  [kernel(): pl.pallas_call(body, out_shape=[jax.ShapeDtypeStruct(shape, dtype) for sh...]
    reduce_sum x137 -> x0, other arithmetic: 18.5 us -> none  [the longest x136 17.7 us: advance(): output = jnp.sum(query_row[:, None] * state, axis=0)]
    mul x561 -> x0, other arithmetic: 18.2 us -> none  [the longest x32 12.7 us: advance(): decay = 1.0 - eps_row[None, :] * (key_row * key_row)[:, None]]
  transfers between devices with their start and end apart: 5 -> 15, of which waited for: 2 -> 7; matrix products, arithmetic and copies ran while one was open for 24% -> 9% of each run, Pallas kernels for 0% -> 10%
where the time goes in v1:
time: 250 us; the launch traced here: 249 us
  waiting for transfers between devices  154 us (62%)
  Pallas kernels  24.2 us (10%)
  starting transfers between devices  18.8 us (8%)
  local copies, waits for them, and re-layouts  17.7 us (7%)
  between operations  13.7 us (5%)
  blocking collectives  8.86 us (4%)
  matrix products  7.74 us (3%)
  other arithmetic  4.46 us (2%)
    all_gather x1, waiting for transfers between devices, per_device(): piece = lax.all_gather(in_weight, 'seq', axis=0, tiled=True)  120 us
    pallas_call x3, Pallas kernels, kernel(): pl.pallas_call(body, out_shape=[jax.ShapeDtypeStruct(shape, dtype) for sh...  24.2 us
    ppermute x7, waiting for transfers between devices, incoming(): lax.ppermute(payload, 'seq', [(i, (i + shift) % count) for i in range(cou...  16.7 us
    ppermute x4, waiting for transfers between devices, swap(): return lax.ppermute(array, axis, [(i, i ^ distance) for i in range(count)])  14.4 us
    unnamed x23, local copies, waits for them, and re-layouts  13.9 us
    ppermute x7, starting transfers between devices, incoming(): lax.ppermute(payload, 'seq', [(i, (i + shift) % count) for i in range(cou...  12.2 us
    all_gather x1, blocking collectives, per_device(): lax.all_gather(hidden_in, 'chan', axis=1, tiled=True).astype(jnp.float32)  8.86 us
  transfers between devices with their start and end apart: 15, of which 7 were waited for; matrix products, arithmetic and copies ran while one was open for 9% of the time, Pallas kernels for 10%

profile of v1, /device:TPU:0, one launch (start us, length us, event | category | flops | bytes accessed | tf_op | source)
XLA Modules:
  0.0 249.3 jit_solution(8118532787607074231)
XLA Ops:
  6.5 0.7 all-gather.3.cloned.1.call-update
  8.0 8.9 %all_gather.9 = bf16[128,2048]{1,0:T(8,128)(2,1)S(1)} all-gather(bf16[128,512]{1,0:T(8,128)(2,1)} %param.10), channel_id=1, replica_groups=mesh['seq'=8,'chan'=4] {'chan'}, dimensions={1}, use_global_device_ids=true | all-gather | bytes 655360 | tf_op jit(solution)/shard_map/all_gather | solution.py:205
  17.1 119.6 %all-gather.3.cloned.1.call-done = bf16[2048,2,1024]{2,1,0:T(2,128)(2,1)} async-done(((bf16[256,2,1024]{2,1,0:T(2,128)(2,1)}), bf16[2048,2,1024]{2,1,0:T(2,128)(2,1)}) %all-gather.3.cloned.1.call-update) | async-done | bytes 8388624 | tf_op jit(solution)/shard_map/all_gather | solution.py:214
  136.7 10.2 %copy.24 = bf16[256,8,2,1024]{3,1,2,0:T(8,128)(2,1)} copy(bf16[256,8,2,1024]{3,2,1,0:T(2,128)(2,1)} %bitcast.48) | data formatting | bytes 16777216
  146.9 4.7 %convolution_convert_fusion = bf16[128,2048]{1,0:T(8,128)(2,1)S(1)} fusion(bf16[2048,2048]{1,0:T(8,128)(2,1)} %bitcast.47, bf16[128,2048]{1,0:T(8,128)(2,1)S(1)} %all_gather.9, f32[2048]{0:T(1024)S(1)} %copy-done.2, f32[128]{0:T(128)S(1)} %add_rsqrt_fusion), kind=kOutput, calls=%fused_computation | convolution fusion | flops 1075052544 | bytes 9445888 | tf_op jit(solution)/shard_map/dot_general | solution.py:215
  152.2 0.8 slice_bitcast_fusion
  153.0 2.6 %collective-permute-start = (bf16[8,3,128]{2,1,0:T(4,128)(2,1)S(1)}, bf16[8,3,128]{2,1,0:T(4,128)(2,1)S(1)}, u32[]{:S(2)}, u32[]{:S(2)}) collective-permute-start(bf16[8,3,128]{2,1,0:T(4,128)(2,1)S(1)} %get-tuple-element.25), channel_id=1, source_target_pairs={{0,4},{4,8},{8,12},{12,16},{16,20},{20,24},{24,28},{1,5},{5,9},{9,... | collective-permute-start | bytes 18440 | tf_op jit(solution)/shard_map/ppermute | solution.py:23
  155.6 1.3 collective-permute-start.1
  158.1 1.3 copy.21
  159.4 1.7 collective-permute-done.1.high
  161.7 2.9 %conv.1 = (bf16[2,8,128,128]{3,2,1,0:T(8,128)(2,1)}, f32[2,128,160]{2,1,0:T(8,128)}) custom-call(bf16[8,128,128]{2,1,0:T(8,128)(2,1)} %copy-done, bf16[8,3,128]{2,1,0:T(4,128)(2,1)} %copy-done.4, bf16[8,3,128]{2,1,0:T(4,128)(2,1)} %copy-done.5, f32[2,4,8,128]{3,2,1,0:T(8,128)} %reshape.55.weight, f32[2,8,128]{2,1,0:T(8,128)} %bitcast.57, ...), custom_call_target="tpu_custom_call" | custom-call | tf_op jit(solution)/shard_map/conv/pallas_call | solution.py:141
  164.6 1.7 collective-permute-done.2
  166.4 1.0 add.126
  167.3 1.5 collective-permute-start.3
  169.5 6.3 %collective-permute-done.3 = f32[2,128,160]{2,1,0:T(8,128)S(1)} collective-permute-done((f32[2,128,160]{2,1,0:T(8,128)S(1)}, f32[2,128,160]{2,1,0:T(8,128)S(1)}, u32[]{:S(2)}, u32[]{:S(2)}) %collective-permute-start.3) | collective-permute-done | bytes 163872 | tf_op jit(solution)/shard_map/ppermute | solution.py:16
  175.8 0.7 add.127.features
  176.5 10.2 %summary.1 = (f32[2,128,8,128]{3,2,1,0:T(8,128)}, f32[2,128,8,128]{3,2,1,0:T(8,128)}, bf16[2,16,8,128]{3,2,1,0:T(8,128)(2,1)}, bf16[2,16,8,128]{3,2,1,0:T(8,128)(2,1)}) custom-call(bf16[2,8,128,128]{3,2,1,0:T(8,128)(2,1)} %get-tuple-element.11.driven, f32[2,128,160]{2,1,0:T(8,128)} %add.127.features, bf16[2,128,1024]{2,1,0:T(8,128)(2,1)} %step_weight.1, ...), custom_call_target="tpu_custom_call" | custom-call | tf_op jit(solution)/shard_map/summary/pallas_call | solution.py:141
  186.7 0.8 select_bitcast_fusion.6
  187.6 2.1 collective-permute-start.10
  189.7 3.0 %collective-permute-start.9 = (bf16[2,16,8,128]{3,2,1,0:T(8,128)(2,1)S(1)}, bf16[2,16,8,128]{3,2,1,0:T(8,128)(2,1)S(1)}, u32[]{:S(2)}, u32[]{:S(2)}) collective-permute-start(bf16[2,16,8,128]{3,2,1,0:T(8,128)(2,1)S(1)} %get-tuple-element.27), channel_id=1, source_target_pairs={{0,24},{4,28},{8,0},{12,4},{16,8},{20,12},{24,16},{28,20},{1,25},{... | collective-permute-start | bytes 196616 | tf_op jit(solution)/shard_map/ppermute | solution.py:158
  192.8 2.1 collective-permute-start.7
  194.9 0.8 collective-permute-start.6
  195.7 2.7 %collective-permute-start.5 = (bf16[2,16,8,128]{3,2,1,0:T(8,128)(2,1)S(1)}, bf16[2,16,8,128]{3,2,1,0:T(8,128)(2,1)S(1)}, u32[]{:S(2)}, u32[]{:S(2)}) collective-permute-start(bf16[2,16,8,128]{3,2,1,0:T(8,128)(2,1)S(1)} %get-tuple-element.26), channel_id=1, source_target_pairs={{0,8},{4,12},{8,16},{12,20},{16,24},{20,28},{24,0},{28,4},{1,9},{5... | collective-permute-start | bytes 196616 | tf_op jit(solution)/shard_map/ppermute | solution.py:158
  198.4 1.4 collective-permute-start.4
  200.5 16.7 %collective-permute-done.7 = bf16[2,16,8,128]{3,2,1,0:T(8,128)(2,1)S(1)} collective-permute-done((bf16[2,16,8,128]{3,2,1,0:T(8,128)(2,1)S(1)}, bf16[2,16,8,128]{3,2,1,0:T(8,128)(2,1)S(1)}, u32[]{:S(2)}, u32[]{:S(2)}) %collective-permute-start.7) | collective-permute-done | bytes 65568 | tf_op jit(solution)/shard_map/ppermute | solution.py:158
  218.1 11.1 %read.1 = bf16[128,1024]{1,0:T(8,128)(2,1)} custom-call(bf16[2,8,128,128]{3,2,1,0:T(8,128)(2,1)} %get-tuple-element.11.driven, f32[2,128,160]{2,1,0:T(8,128)} %add.127.features, f32[2,128,8,128]{3,2,1,0:T(8,128)} %get-tuple-element.13.eps, f32[2,128,8,128]{3,2,1,0:T(8,128)} %get-tuple-element.14.drive, f32[2,16,8,128]{3,2,1,0:T(8,128)} %pad_maximum_fusion.initial, ...), custom_call_target="tpu_custom_call" | custom-call | tf_op jit(solution)/shard_map/read/pallas_call | solution.py:141
  229.1 3.0 %fusion.10 = f32[128,2048]{1,0:T(8,128)S(1)} fusion(bf16[128,1024]{1,0:T(8,128)(2,1)} %read.1, bf16[1024,2048]{1,0:T(8,128)(2,1)} %all-gather.5.cloned.1.call-done), kind=kOutput, calls=%fused_computation.36 | convolution fusion | flops 536870912 | bytes 5505024 | tf_op jit(solution)/shard_map/dot_general | solution.py:257
  232.1 0.9 reshape_reshape.3
  233.0 0.9 constant_dynamic-slice_fusion.1
  234.2 1.9 collective-permute-done.11
  236.2 1.1 collective-permute-start.12
  237.3 4.5 %collective-permute-done.12 = bf16[128,1,512]{2,0,1:T(8,128)(2,1)S(1)} collective-permute-done((bf16[128,1,512]{2,0,1:T(8,128)(2,1)S(1)}, bf16[128,1,512]{2,0,1:T(8,128)(2,1)S(1)}, u32[]{:S(2)}, u32[]{:S(2)}) %collective-permute-start.12) | collective-permute-done | bytes 131104 | tf_op jit(solution)/shard_map/ppermute | solution.py:16
  (56 shorter events, 6.5 us)
Async XLA Ops:
  6.5 130.2 %all-gather.3.cloned.1.call-start = ((), (), s32[]{:S(2)}) async-start(), calls=%async_computation | async-start | bytes 9437184 | tf_op jit(solution)/shard_map/all_gather | solution.py:214
  7.3 221.9 %all-gather.5.cloned.1.call-start = ((), (), s32[]{:S(2)}) async-start(), calls=%async_computation.1 | async-start | bytes 4718592 | tf_op jit(solution)/shard_map/all_gather | solution.py:259
  136.7 10.2 %copy-start.2 = (f32[2048]{0:T(1024)S(1)}, f32[2048]{0:T(1024)}, u32[]{:S(2)}) copy-start(f32[2048]{0:T(1024)} %param.11) | copy-start | bytes 24580
  146.9 10.0 %copy-start.3 = (f32[2,4,1024]{2,1,0:T(4,128)S(1)}, f32[2,4,1024]{2,1,0:T(4,128)}, u32[]{:S(2)}) copy-start(f32[2,4,1024]{2,1,0:T(4,128)} %param.13) | copy-start | bytes 98308
  146.9 10.6 %copy-start.6 = (f32[2,1024]{1,0:T(2,128)S(1)}, f32[2,1024]{1,0:T(2,128)}, u32[]{:S(2)}) copy-start(f32[2,1024]{1,0:T(2,128)} %param.14) | copy-start | bytes 24580
  146.9 11.2 %copy-start.1 = (bf16[2,1024,160]{1,2,0:T(8,128)(2,1)S(1)}, bf16[2,1024,160]{1,2,0:T(8,128)(2,1)}, u32[]{:S(2)}) copy-start(bf16[2,1024,160]{1,2,0:T(8,128)(2,1)} %param.15) | copy-start | bytes 1966084
  146.9 22.0 %copy-start.7 = (f32[2,1024]{1,0:T(2,128)S(1)}, f32[2,1024]{1,0:T(2,128)}, u32[]{:S(2)}) copy-start(f32[2,1024]{1,0:T(2,128)} %param.17) | copy-start | bytes 24580
  151.6 48.2 %copy-start.8 = (f32[2,1024]{1,0:T(2,128)S(1)}, f32[2,1024]{1,0:T(2,128)}, u32[]{:S(2)}) copy-start(f32[2,1024]{1,0:T(2,128)} %param.18) | copy-start | bytes 24580
  153.0 8.1 %copy-start = (bf16[8,128,128]{2,1,0:T(8,128)(2,1)}, bf16[8,128,128]{2,1,0:T(8,128)(2,1)S(1)}, u32[]{:S(2)}) copy-start(bf16[8,128,128]{2,1,0:T(8,128)(2,1)S(1)} %get-tuple-element.23.branch) | copy-start | bytes 786436
  153.0 6.4 %collective-permute-start = (bf16[8,3,128]{2,1,0:T(4,128)(2,1)S(1)}, bf16[8,3,128]{2,1,0:T(4,128)(2,1)S(1)}, u32[]{:S(2)}, u32[]{:S(2)}) collective-permute-start(bf16[8,3,128]{2,1,0:T(4,128)(2,1)S(1)} %get-tuple-element.25), channel_id=1, source_target_pairs={{0,4},{4,8},{8,12},{12,16},{16,20},{20,24},{24,28},{1,5},{5,9},{9,... | collective-permute-start | bytes 18440 | tf_op jit(solution)/shard_map/ppermute | solution.py:23
  155.6 5.5 %collective-permute-start.1 = (bf16[8,3,128]{2,1,0:T(4,128)(2,1)S(1)}, bf16[8,3,128]{2,1,0:T(4,128)(2,1)S(1)}, u32[]{:S(2)}, u32[]{:S(2)}) collective-permute-start(bf16[8,3,128]{2,1,0:T(4,128)(2,1)S(1)} %get-tuple-element.24), channel_id=1, source_target_pairs={{4,0},{8,4},{12,8},{16,12},{20,16},{24,20},{28,24},{5,1},{9,5},{13... | collective-permute-start | bytes 18440 | tf_op jit(solution)/shard_map/ppermute | solution.py:24
  159.4 1.7 copy-start.4
  161.1 0.6 copy-start.5
  164.6 1.7 collective-permute-start.2
  167.3 8.4 %collective-permute-start.3 = (f32[2,128,160]{2,1,0:T(8,128)S(1)}, f32[2,128,160]{2,1,0:T(8,128)S(1)}, u32[]{:S(2)}, u32[]{:S(2)}) collective-permute-start(f32[2,128,160]{2,1,0:T(8,128)S(1)} %add.126), channel_id=1, source_target_pairs={{0,2},{1,3},{2,0},{3,1},{4,6},{5,7},{6,4},{7,5},{8,10},{9,11},{10,... | collective-permute-start | bytes 491528 | tf_op jit(solution)/shard_map/ppermute | solution.py:16
  187.6 8.1 %collective-permute-start.10 = (bf16[2,16,8,128]{3,2,1,0:T(8,128)(2,1)S(1)}, bf16[2,16,8,128]{3,2,1,0:T(8,128)(2,1)S(1)}, u32[]{:S(2)}, u32[]{:S(2)}) collective-permute-start(bf16[2,16,8,128]{3,2,1,0:T(8,128)(2,1)S(1)} %get-tuple-element.31), channel_id=1, source_target_pairs={{0,28},{4,0},{8,4},{12,8},{16,12},{20,16},{24,20},{28,24},{1,29},{... | collective-permute-start | bytes 196616 | tf_op jit(solution)/shard_map/ppermute | solution.py:158
  189.7 8.6 %collective-permute-start.9 = (bf16[2,16,8,128]{3,2,1,0:T(8,128)(2,1)S(1)}, bf16[2,16,8,128]{3,2,1,0:T(8,128)(2,1)S(1)}, u32[]{:S(2)}, u32[]{:S(2)}) collective-permute-start(bf16[2,16,8,128]{3,2,1,0:T(8,128)(2,1)S(1)} %get-tuple-element.27), channel_id=1, source_target_pairs={{0,24},{4,28},{8,0},{12,4},{16,8},{20,12},{24,16},{28,20},{1,25},{... | collective-permute-start | bytes 196616 | tf_op jit(solution)/shard_map/ppermute | solution.py:158
  192.8 7.7 %collective-permute-start.8 = (bf16[2,16,8,128]{3,2,1,0:T(8,128)(2,1)S(1)}, bf16[2,16,8,128]{3,2,1,0:T(8,128)(2,1)S(1)}, u32[]{:S(2)}, u32[]{:S(2)}) collective-permute-start(bf16[2,16,8,128]{3,2,1,0:T(8,128)(2,1)S(1)} %get-tuple-element.28), channel_id=1, source_target_pairs={{0,20},{4,24},{8,28},{12,0},{16,4},{20,8},{24,12},{28,16},{1,21},{... | collective-permute-start | bytes 196616 | tf_op jit(solution)/shard_map/ppermute | solution.py:158
  192.8 24.4 %collective-permute-start.7 = (bf16[2,16,8,128]{3,2,1,0:T(8,128)(2,1)S(1)}, bf16[2,16,8,128]{3,2,1,0:T(8,128)(2,1)S(1)}, u32[]{:S(2)}, u32[]{:S(2)}) collective-permute-start(bf16[2,16,8,128]{3,2,1,0:T(8,128)(2,1)S(1)} %get-tuple-element.29), channel_id=1, source_target_pairs={{0,16},{4,20},{8,24},{12,28},{16,0},{20,4},{24,8},{28,12},{1,17},{... | collective-permute-start | bytes 196616 | tf_op jit(solution)/shard_map/ppermute | solution.py:158
  194.9 22.3 %collective-permute-start.6 = (bf16[2,16,8,128]{3,2,1,0:T(8,128)(2,1)S(1)}, bf16[2,16,8,128]{3,2,1,0:T(8,128)(2,1)S(1)}, u32[]{:S(2)}, u32[]{:S(2)}) collective-permute-start(bf16[2,16,8,128]{3,2,1,0:T(8,128)(2,1)S(1)} %get-tuple-element.30), channel_id=1, source_target_pairs={{0,12},{4,16},{8,20},{12,24},{16,28},{20,0},{24,4},{28,8},{1,13},{... | collective-permute-start | bytes 196616 | tf_op jit(solution)/shard_map/ppermute | solution.py:158
  195.7 21.5 %collective-permute-start.5 = (bf16[2,16,8,128]{3,2,1,0:T(8,128)(2,1)S(1)}, bf16[2,16,8,128]{3,2,1,0:T(8,128)(2,1)S(1)}, u32[]{:S(2)}, u32[]{:S(2)}) collective-permute-start(bf16[2,16,8,128]{3,2,1,0:T(8,128)(2,1)S(1)} %get-tuple-element.26), channel_id=1, source_target_pairs={{0,8},{4,12},{8,16},{12,20},{16,24},{20,28},{24,0},{28,4},{1,9},{5... | collective-permute-start | bytes 196616 | tf_op jit(solution)/shard_map/ppermute | solution.py:158
  198.4 18.9 %collective-permute-start.4 = (bf16[2,16,8,128]{3,2,1,0:T(8,128)(2,1)S(1)}, bf16[2,16,8,128]{3,2,1,0:T(8,128)(2,1)S(1)}, u32[]{:S(2)}, u32[]{:S(2)}) collective-permute-start(bf16[2,16,8,128]{3,2,1,0:T(8,128)(2,1)S(1)} %get-tuple-element.17), channel_id=1, source_target_pairs={{0,4},{4,8},{8,12},{12,16},{16,20},{20,24},{24,28},{28,0},{1,5},{5... | collective-permute-start | bytes 196616 | tf_op jit(solution)/shard_map/ppermute | solution.py:158
  234.0 2.0 collective-permute-start.11
  236.2 5.6 %collective-permute-start.12 = (bf16[128,1,512]{2,0,1:T(8,128)(2,1)S(1)}, bf16[128,1,512]{2,0,1:T(8,128)(2,1)S(1)}, u32[]{:S(2)}, u32[]{:S(2)}) collective-permute-start(bf16[128,1,512]{2,0,1:T(8,128)(2,1)S(1)} %dynamic-slice_convert_fusion), channel_id=1, source_target_pairs={{0,2},{1,3},{2,0},{3,1},{4,6},{5,7},{6,4},{7,5},{8,10},{9,11},{10,... | collective-permute-start | bytes 393224 | tf_op jit(solution)/shard_map/ppermute | solution.py:16
Sparse Core Ops, SparseCore 0:
  9.5 127.1 all-gather.2
  138.7 82.6 all-gather.4
